TPU v7x, 32 devices: a whole 2x2x4 slice. The times are simulated.
32 devices in a mesh: dom: 16 (over z, y, x), col: 2 (over core).
Axes of the slice: x: 2, y: 2, z: 4, core: 2. Of those that a mesh axis runs over, the one named last changes fastest.
Arguments:
- features: bfloat16 [16384, 256], P(('dom', 'col')), may hold values from -6 to 6
- weight: bfloat16 [256, 256], replicated, may hold values from -0.375 to 0.375
- cotangent: bfloat16 [16384, 256], P(('dom', 'col')), may hold values from -6 to 6
- tile_values: bfloat16 [1280, 128, 128], P(('dom', 'col')), may hold values from -0.15625 to 0.15625
- tile_rows: int32 [1280], P(('dom', 'col')), may hold values from 0 to 7
- tile_cols: int32 [1280], P(('dom', 'col')), may hold values from 0 to 19, as said below
- tile_count: int32 [32], P(('dom', 'col')), may hold values from 20 to 40, as said below
- send_blocks: int32 [32, 16], P(('dom', 'col')), may hold values from 0 to 3
Outputs:
- output_rows: bfloat16 [16384, 256], P(('dom', 'col'))
- feature_grad: bfloat16 [16384, 256], P(('dom', 'col'))
- weight_grad: float32 [256, 256], replicated
Inputs may be any that keep to these rules, and one draw needn't show every extreme that they name: `tile_cols`: A value v below 4 names the device's own row block v; a value 4 + s names the row block that the device of partition s with the same col index sends to this partition; no receive slot is named by two tiles of one device. Only the first tile_count slots of a device's tiles are live; some device has all 40 live.
All inputs are finite; a program needn't handle non-finite values.
Results may differ from a plain program's by a relative error of at most 0.0049.
Values may be sent and summed in bfloat16 or wider, within the bound.
A program may use at most 128 MiB of HBM per device.

v0:
```python
import jax
import jax.numpy as jnp
from jax import lax
from jax.sharding import PartitionSpec as P


def local(features, weight, cotangent, tile_values, tile_rows, tile_cols, tile_count, send_blocks):
    block_size = tile_values.shape[1]
    half_blocks = features.shape[0] // block_size
    width_in = features.shape[1]
    peer_count = send_blocks.shape[1]
    all_blocks = half_blocks * lax.axis_size("col")
    node_total = features.shape[0] * lax.axis_size("col") * lax.axis_size("dom")
    own_blocks = features.reshape(half_blocks, block_size, width_in)
    outgoing = own_blocks[send_blocks[0]]
    incoming = lax.all_to_all(outgoing, "dom", split_axis=0, concat_axis=0, tiled=True)
    sources = jnp.concatenate([own_blocks, incoming], axis=0)
    live_bool = jnp.arange(tile_values.shape[0], dtype=jnp.int32) < tile_count[0]
    live_mask = live_bool.astype(jnp.bfloat16)
    masked_tiles = tile_values * live_mask[:, None, None]
    picked = sources[tile_cols]
    products = jnp.einsum("tij,tjf->tif", masked_tiles, picked, preferred_element_type=jnp.float32)
    partial_value = jax.ops.segment_sum(products, tile_rows, num_segments=all_blocks)
    summed = lax.psum_scatter(partial_value, "col", scatter_dimension=0, tiled=True)
    hidden = summed.astype(jnp.bfloat16).reshape(half_blocks * block_size, width_in)
    output_rows = jnp.dot(hidden, weight, preferred_element_type=jnp.float32).astype(jnp.bfloat16)
    own_grad = lax.dot_general(
        cotangent, weight, (((1,), (1,)), ((), ())), preferred_element_type=jnp.float32
    ).astype(jnp.bfloat16)
    own_grad = own_grad.reshape(half_blocks, block_size, width_in)
    grad_blocks = lax.all_gather(own_grad, "col", axis=0, tiled=True)
    chosen = grad_blocks[tile_rows]
    back_terms = jnp.einsum(
        "tji,tjf->tif", masked_tiles, chosen, preferred_element_type=jnp.float32
    )
    spread = jax.ops.segment_sum(back_terms, tile_cols, num_segments=half_blocks + peer_count)
    returned = lax.all_to_all(spread[half_blocks:], "dom", split_axis=0, concat_axis=0, tiled=True)
    grad_total = spread[:half_blocks] + jax.ops.segment_sum(
        returned, send_blocks[0], num_segments=half_blocks
    )
    feature_grad = grad_total.astype(jnp.bfloat16).reshape(half_blocks * block_size, width_in)
    local_weight = lax.dot_general(
        hidden, cotangent, (((0,), (0,)), ((), ())), preferred_element_type=jnp.float32
    )
    local_weight = local_weight * jnp.float32(1.0 / node_total**0.5)
    col_share = lax.psum_scatter(local_weight, "col", scatter_dimension=0, tiled=True)
    dom_share = lax.psum(col_share, "dom")
    weight_grad = lax.all_gather(dom_share, "col", axis=0, tiled=True)
    return (output_rows, feature_grad, weight_grad)


def solution(mesh):
    return jax.shard_map(
        local,
        mesh=mesh,
        in_specs=(
            P(("dom", "col"), None),
            P(),
            P(("dom", "col"), None),
            P(("dom", "col"), None, None),
            P(("dom", "col")),
            P(("dom", "col")),
            P(("dom", "col")),
            P(("dom", "col"), None),
        ),
        out_specs=(P(("dom", "col"), None), P(("dom", "col"), None), P()),
        check_vma=False,
    )
```

profile of v0, /device:TPU:0, one launch (start us, length us, event | category | flops | bytes accessed | tf_op | source)
XLA Modules:
  0.0 214.5 jit_solution(6143368337666922137)
XLA Ops:
  7.2 0.0 copy-start
  7.2 0.0 copy-start.7
  7.2 0.0 copy-start.5
  7.2 0.7 fusion.6
  7.9 2.6 %gather_fusion = bf16[16,128,256]{2,1,0:T(8,128)(2,1)} fusion(bf16[4,128,256]{2,1,0:T(8,128)(2,1)} %bitcast.19, s32[1024]{0:T(1024)S(1)} %pad_clamp_fusion.2), kind=kCustom, calls=%fused_computation | custom fusion | bytes 2097216 | tf_op jit(solution)/shard_map/gather | solution.py:15
  10.5 8.4 %all-to-all-start = ((bf16[16,128,256]{2,1,0:T(8,128)(2,1)}), bf16[16,128,256]{2,1,0:T(8,128)(2,1)}, u32[]{:S(2)}, u32[]{:S(2)}) async-start(bf16[16,128,256]{2,1,0:T(8,128)(2,1)} %gather_fusion), calls=%async_computation | async-start | bytes 2097152 | tf_op jit(solution)/shard_map/all_to_all | solution.py:16
  19.5 0.0 copy-done.7
  19.6 0.0 copy-done
  19.6 0.0 copy-done.5
  19.6 0.3 convolution_convert_fusion
  19.9 2.2 %all_gather.6 = bf16[8,128,256]{2,1,0:T(8,128)(2,1)S(1)} all-gather(bf16[4,128,256]{2,1,0:T(8,128)(2,1)S(1)} %bitcast.23), channel_id=1, replica_groups=mesh['dom'=16,'col'=2] {'col'}, dimensions={0}, use_global_device_ids=true | all-gather | bytes 786432 | tf_op jit(solution)/shard_map/all_gather | solution.py:31
  22.0 0.7 gather_fusion.2
  22.8 4.9 %fusion = f32[40,128,256]{2,1,0:T(8,128)} fusion(bf16[40,128,256]{2,1,0:T(8,128)(2,1)S(1)} %gather_fusion.2, bf16[40,128,128]{2,1,0:T(8,128)(2,1)} %param.11, bf16[40]{0:T(256)(128)(2,1)S(1)} %compare_convert_fusion), kind=kOutput, calls=%fused_computation.10 | convolution fusion | flops 336199680 | bytes 9175120 | tf_op jit(solution)/shard_map/tji,tjf->tif/dot_general | solution.py:33
  27.7 0.0 copy-start.6
  27.7 0.3 broadcast_in_dim.24
  28.0 0.4 copy-done.6
  28.4 9.1 %scatter_fusion.1 = f32[20,128,256]{2,1,0:T(8,128)S(1)} fusion(f32[20,128,256]{2,1,0:T(8,128)S(1)} %broadcast_in_dim.24, s32[40]{0:T(128)S(1)} %copy-done.6, f32[40,128,256]{2,1,0:T(8,128)} %fusion), kind=kCustom, calls=%fused_computation.4 | custom fusion | flops 1310720 | bytes 15728800 | tf_op jit(solution)/shard_map/scatter-add | solution.py:36
  37.4 0.0 copy-start.2
  37.4 1.8 slice.15
  39.2 0.0 copy-start.3
  39.2 4.1 %all-to-all-done = bf16[16,128,256]{2,1,0:T(8,128)(2,1)} async-done(((bf16[16,128,256]{2,1,0:T(8,128)(2,1)}), bf16[16,128,256]{2,1,0:T(8,128)(2,1)}, u32[]{:S(2)}, u32[]{:S(2)}) %all-to-all-start) | async-done | bytes 1048608 | tf_op jit(solution)/shard_map/all_to_all | solution.py:16
  43.3 0.0 copy-done.2
  43.3 5.9 %all-to-all-start.1 = ((f32[16,128,256]{2,1,0:T(8,128)}), f32[16,128,256]{2,1,0:T(8,128)}, u32[]{:S(2)}, u32[]{:S(2)}) async-start(f32[16,128,256]{2,1,0:T(8,128)} %slice.15), calls=%async_computation.2 | async-start | bytes 4194304 | tf_op jit(solution)/shard_map/all_to_all | solution.py:37
  49.3 0.0 reduce-scatter.3.cloned.1.call-start
  49.3 0.0 copy-done.3
  49.4 1.3 pad_maximum_fusion
  50.7 0.0 copy-start.4
  50.7 2.4 %gather_fusion.1 = bf16[40,128,256]{2,1,0:T(8,128)(2,1)} fusion(bf16[20,128,256]{2,1,0:T(8,128)(2,1)S(1)} %pad_maximum_fusion, s32[1024]{0:T(1024)S(1)} %pad_clamp_fusion.1), kind=kCustom, calls=%fused_computation.1 | custom fusion | bytes 5243040 | tf_op jit(solution)/shard_map/gather | solution.py:21
  53.1 0.0 copy-done.4
  53.1 4.9 %fusion.2 = f32[40,128,256]{2,1,0:T(8,128)} fusion(bf16[40,128,256]{2,1,0:T(8,128)(2,1)} %gather_fusion.1, bf16[40,128,128]{2,1,0:T(8,128)(2,1)S(1)} %copy-done.4, bf16[40]{0:T(256)(128)(2,1)S(1)} %compare_convert_fusion), kind=kOutput, calls=%fused_computation.12 | convolution fusion | flops 336199680 | bytes 9175120 | tf_op jit(solution)/shard_map/tij,tjf->tif/dot_general | solution.py:22
  58.1 0.1 broadcast_in_dim.21
  58.1 9.0 %scatter_fusion = f32[8,128,256]{2,1,0:T(8,128)S(1)} fusion(f32[8,128,256]{2,1,0:T(8,128)S(1)} %broadcast_in_dim.21, s32[40]{0:T(128)S(1)} %copy-done.7, f32[40,128,256]{2,1,0:T(8,128)} %fusion.2), kind=kCustom, calls=%fused_computation.3 | custom fusion | flops 1310720 | bytes 15728800 | tf_op jit(solution)/shard_map/scatter-add | solution.py:23
  67.2 0.0 copy-start.1
  67.2 0.0 copy-start.8
  67.2 1.1 copy-done.1
  68.3 0.0 reduce-scatter.3.cloned.1.call-update
  68.3 0.0 reduce-scatter.5.cloned.1.call-start
  68.4 9.7 %reduce-scatter.3.cloned.1.call-done = f32[4,128,256]{2,1,0:T(8,128)} async-done(((f32[8,128,256]{2,1,0:T(8,128)}), f32[4,128,256]{2,1,0:T(8,128)}) %reduce-scatter.3.cloned.1.call-update) | async-done | bytes 524304 | tf_op jit(solution)/shard_map/reduce_scatter | solution.py:24
  78.1 1.1 convert_element_type.20
  79.1 1.0 convolution_multiply_fusion
  80.1 0.0 reduce-scatter.5.cloned.1.call-update
  80.1 0.0 all-reduce.2.cloned.1.call-start
  80.2 1.1 slice.14
  81.3 10.0 %all-to-all-done.1 = f32[16,128,256]{2,1,0:T(8,128)} async-done(((f32[16,128,256]{2,1,0:T(8,128)}), f32[16,128,256]{2,1,0:T(8,128)}, u32[]{:S(2)}, u32[]{:S(2)}) %all-to-all-start.1) | async-done | bytes 2097184 | tf_op jit(solution)/shard_map/all_to_all | solution.py:37
  91.2 0.0 copy-done.8
  91.2 3.5 %scatter_fusion.2 = f32[4,128,256]{2,1,0:T(8,128)S(1)} fusion(f32[4,128,256]{2,1,0:T(8,128)S(1)} %slice.14, s32[16]{0:T(128)S(1)} %bitcast.25, f32[16,128,256]{2,1,0:T(8,128)} %all-to-all-done.1), kind=kCustom, calls=%fused_computation.5 | custom fusion | flops 524288 | bytes 6291520 | tf_op jit(solution)/shard_map/scatter-add | solution.py:38
  94.7 0.7 convert_element_type.23
  95.4 0.0 reduce-scatter.5.cloned.1.call-done
  95.4 0.0 all-reduce.2.cloned.1.call-update
  95.5 0.9 convolution_convert_fusion.1
  96.4 108.7 %all-reduce.2.cloned.1.call-done = f32[128,256]{1,0:T(8,128)} async-done(((f32[128,256]{1,0:T(8,128)}), f32[128,256]{1,0:T(8,128)}) %all-reduce.2.cloned.1.call-update) | async-done | bytes 131088 | tf_op jit(solution)/shard_map/psum | solution.py:47
  205.1 2.2 %all_gather.7 = f32[256,256]{1,0:T(8,128)S(1)} all-gather(f32[128,256]{1,0:T(8,128)} %all-reduce.2.cloned.1.call-done), channel_id=1, replica_groups=mesh['dom'=16,'col'=2] {'col'}, dimensions={0}, use_global_device_ids=true | all-gather | bytes 393216 | tf_op jit(solution)/shard_map/all_gather | solution.py:48
  207.3 0.7 copy.20
  (6 shorter events, 0.0 us)
Async XLA Ops:
  7.2 12.4 %copy-start = (bf16[512,256]{1,0:T(8,128)(2,1)S(1)}, bf16[512,256]{1,0:T(8,128)(2,1)}, u32[]{:S(2)}) copy-start(bf16[512,256]{1,0:T(8,128)(2,1)} %param.10) | copy-start | bytes 786436
  7.2 12.4 %copy-start.7 = (s32[40]{0:T(128)S(1)}, s32[40]{0:T(128)}, u32[]{:S(2)}) copy-start(s32[40]{0:T(128)} %param.12) | copy-start | bytes 484
  7.2 12.4 %copy-start.5 = (bf16[256,256]{1,0:T(8,128)(2,1)S(1)}, bf16[256,256]{1,0:T(8,128)(2,1)}, u32[]{:S(2)}) copy-start(bf16[256,256]{1,0:T(8,128)(2,1)} %param.9) | copy-start | bytes 393220
  10.5 32.8 %all-to-all-start = ((bf16[16,128,256]{2,1,0:T(8,128)(2,1)}), bf16[16,128,256]{2,1,0:T(8,128)(2,1)}, u32[]{:S(2)}, u32[]{:S(2)}) async-start(bf16[16,128,256]{2,1,0:T(8,128)(2,1)} %gather_fusion), calls=%async_computation | async-start | bytes 2097152 | tf_op jit(solution)/shard_map/all_to_all | solution.py:16
  27.7 0.7 copy-start.6
  37.4 5.9 %copy-start.2 = (f32[20,128,256]{2,1,0:T(8,128)}, f32[20,128,256]{2,1,0:T(8,128)S(1)}, u32[]{:S(2)}) copy-start(f32[20,128,256]{2,1,0:T(8,128)S(1)} %scatter_fusion.1) | copy-start | bytes 7864324
  39.2 10.1 %copy-start.3 = (bf16[512,256]{1,0:T(8,128)(2,1)S(1)}, bf16[512,256]{1,0:T(8,128)(2,1)}, u32[]{:S(2)}) copy-start(bf16[512,256]{1,0:T(8,128)(2,1)} %param.8) | copy-start | bytes 786436
  43.3 47.9 %all-to-all-start.1 = ((f32[16,128,256]{2,1,0:T(8,128)}), f32[16,128,256]{2,1,0:T(8,128)}, u32[]{:S(2)}, u32[]{:S(2)}) async-start(f32[16,128,256]{2,1,0:T(8,128)} %slice.15), calls=%async_computation.2 | async-start | bytes 4194304 | tf_op jit(solution)/shard_map/all_to_all | solution.py:37
  49.3 28.8 %reduce-scatter.3.cloned.1.call-start = ((), (), s32[]{:S(2)}) async-start(), calls=%async_computation.4 | async-start | bytes 1572864 | tf_op jit(solution)/shard_map/reduce_scatter | solution.py:24
  50.7 2.4 %copy-start.4 = (bf16[40,128,128]{2,1,0:T(8,128)(2,1)S(1)}, bf16[40,128,128]{2,1,0:T(8,128)(2,1)}, u32[]{:S(2)}) copy-start(bf16[40,128,128]{2,1,0:T(8,128)(2,1)} %param.11) | copy-start | bytes 3932164
  67.2 1.1 copy-start.1
  67.2 24.0 %copy-start.8 = (s32[1,16]{1,0:T(1,128)S(1)}, s32[1,16]{1,0:T(1,128)}, u32[]{:S(2)}) copy-start(s32[1,16]{1,0:T(1,128)} %param.15) | copy-start | bytes 196
  68.3 27.1 %reduce-scatter.5.cloned.1.call-start = ((), (), s32[]{:S(2)}) async-start(), calls=%async_computation.5 | async-start | bytes 393216 | tf_op jit(solution)/shard_map/reduce_scatter | solution.py:46
  80.1 125.0 %all-reduce.2.cloned.1.call-start = ((), (), s32[]{:S(2)}) async-start(), calls=%async_computation.6 | async-start | bytes 262144 | tf_op jit(solution)/shard_map/psum | solution.py:47
Sparse Core Ops, SparseCore 0:
  68.4 9.5 reduce-scatter.2
  80.9 8.9 reduce-scatter.4
  95.6 109.4 all-reduce.1
where the time goes:
time: 215 us
  waiting for transfers between devices  133 us (62%)
  other arithmetic  25.5 us (12%)
  between operations  14.6 us (7%)
  starting transfers between devices  14.4 us (7%)
  matrix products  12 us (6%)
  local copies, waits for them, and re-layouts  11.1 us (5%)
  blocking collectives  4.37 us (2%)
    psum x1, waiting for transfers between devices, local(): dom_share = lax.psum(col_share, 'dom')  109 us
    all_to_all x1, waiting for transfers between devices, local(): lax.all_to_all(spread[half_blocks:], 'dom', split_axis=0, concat_axis=0,...  9.95 us
    reduce_scatter x1, waiting for transfers between devices, local(): lax.psum_scatter(partial_value, 'col', scatter_dimension=0, tiled=True)  9.71 us
    scatter-add x1, other arithmetic, local(): jax.ops.segment_sum(back_terms, tile_cols, num_segments=half_blocks + pee...  9.08 us
    scatter-add x1, other arithmetic, local(): jax.ops.segment_sum(products, tile_rows, num_segments=all_blocks)  9.04 us
    all_to_all x1, starting transfers between devices, local(): lax.all_to_all(outgoing, 'dom', split_axis=0, concat_axis=0, tiled=True)  8.39 us
    all_to_all x1, starting transfers between devices, local(): lax.all_to_all(spread[half_blocks:], 'dom', split_axis=0, concat_axis=0,...  5.93 us
    dot_general x1, matrix products, local(): jnp.einsum('tij,tjf->tif', masked_tiles, picked, preferred_element_type=j...  4.93 us
  transfers between devices with their start and end apart: 5, of which 4 were waited for; matrix products, arithmetic and copies ran while one was open for 20% of the time, Pallas kernels for 0%

commit v1 on v0

--- a/solution.py
+++ b/solution.py
@@ -1,7 +1,44 @@
+import functools
 import jax
 import jax.numpy as jnp
 from jax import lax
 from jax.sharding import PartitionSpec as P
+
+
+def proceed_orders_all(incoming_x, where_dim, my_tile):
+    f_now = incoming_x.shape
+    kept_arr = jnp.moveaxis(
+        incoming_x.reshape(
+            *f_now[:where_dim], my_tile, f_now[where_dim] // my_tile, *f_now[where_dim + 1 :]
+        ),
+        where_dim,
+        0,
+    )
+    return kept_arr
+
+
+def rails_play(arr, ndim_at):
+    arr = jnp.moveaxis(arr, 0, ndim_at)
+    moved = arr.shape
+    m_next = arr.reshape(
+        *moved[:ndim_at], moved[ndim_at] * moved[ndim_at + 1], *moved[ndim_at + 2 :]
+    )
+    return m_next
+
+
+def show_flows(target, group_axis, page, block_in):
+    a_next, carry_in = (lax.psum(1, group_axis), lax.axis_index(group_axis))
+    q_next = proceed_orders_all(target, page, a_next)
+    grid = [q_next[carry_in]]
+    for j0 in range(1, a_next):
+        v1 = q_next[carry_in ^ j0]
+        grid.append(lax.ppermute(v1, group_axis, [(dd, dd ^ j0) for dd in range(a_next)]))
+    q_next = jnp.stack(grid)[carry_in ^ jnp.arange(a_next)]
+    current_value = rails_play(q_next, block_in)
+    return current_value
+
+
+touch_the_case = functools.partial(show_flows, group_axis="dom", page=0, block_in=0)
 
 
 def local(features, weight, cotangent, tile_values, tile_rows, tile_cols, tile_count, send_blocks):
@@ -34,7 +71,7 @@
         "tji,tjf->tif", masked_tiles, chosen, preferred_element_type=jnp.float32
     )
     spread = jax.ops.segment_sum(back_terms, tile_cols, num_segments=half_blocks + peer_count)
-    returned = lax.all_to_all(spread[half_blocks:], "dom", split_axis=0, concat_axis=0, tiled=True)
+    returned = touch_the_case(spread[half_blocks:])
     grad_total = spread[:half_blocks] + jax.ops.segment_sum(
         returned, send_blocks[0], num_segments=half_blocks
     )

time: 215 us -> 247 us (1.15)
  starting transfers between devices: 14.4 us -> 43.2 us
  local copies, waits for them, and re-layouts: 11.1 us -> 32.7 us
  waiting for transfers between devices: 133 us -> 115 us
    ppermute x0 -> x15, starting transfers between devices: none -> 34.5 us  [show_flows(): lax.ppermute(v1, group_axis, [(dd, dd ^ j0) for dd in range(a_next)])]
    unnamed x19 -> x46, local copies, waits for them, and re-layouts: 2.2 us -> 19.3 us
    all_to_all x1 -> x0, waiting for transfers between devices: 9.95 us -> none  [local(): lax.all_to_all(spread[half_blocks:], 'dom', split_axis=0, concat_axis=0,...]
    reduce_scatter x1, waiting for transfers between devices: 9.71 us -> 0.01 us  [local(): lax.psum_scatter(partial_value, 'col', scatter_dimension=0, tiled=True)]
    all_to_all x1 -> x0, starting transfers between devices: 5.93 us -> none  [local(): lax.all_to_all(spread[half_blocks:], 'dom', split_axis=0, concat_axis=0,...]
    all_to_all x1, waiting for transfers between devices: 4.13 us -> 0.01 us  [local(): lax.all_to_all(outgoing, 'dom', split_axis=0, concat_axis=0, tiled=True)]
    ppermute x0 -> x15, waiting for transfers between devices: none -> 3.65 us  [show_flows(): lax.ppermute(v1, group_axis, [(dd, dd ^ j0) for dd in range(a_next)])]
    squeeze x0 -> x1, local copies, waits for them, and re-layouts: none -> 2.82 us  [show_flows(): v1 = q_next[carry_in ^ j0]]
  transfers between devices with their start and end apart: 5 -> 19, of which waited for: 4 -> 4; matrix products, arithmetic and copies ran while one was open for 20% -> 26% of each run, Pallas kernels for 0% -> 0%
where the time goes in v1:
time: 247 us
  waiting for transfers between devices  115 us (47%)
  starting transfers between devices  43.2 us (17%)
  local copies, waits for them, and re-layouts  32.7 us (13%)
  other arithmetic  24.2 us (10%)
  between operations  14.7 us (6%)
  matrix products  12.1 us (5%)
  blocking collectives  4.37 us (2%)
    psum x1, waiting for transfers between devices, local(): dom_share = lax.psum(col_share, 'dom')  111 us
    ppermute x15, starting transfers between devices, show_flows(): lax.ppermute(v1, group_axis, [(dd, dd ^ j0) for dd in range(a_next)])  34.5 us
    unnamed x46, local copies, waits for them, and re-layouts  19.3 us
    scatter-add x1, other arithmetic, local(): jax.ops.segment_sum(back_terms, tile_cols, num_segments=half_blocks + pee...  9.08 us
    scatter-add x1, other arithmetic, local(): jax.ops.segment_sum(products, tile_rows, num_segments=all_blocks)  9.04 us
    all_to_all x1, starting transfers between devices, local(): lax.all_to_all(outgoing, 'dom', split_axis=0, concat_axis=0, tiled=True)  8.52 us
    dot_general x1, matrix products, local(): jnp.einsum('tij,tjf->tif', masked_tiles, picked, preferred_element_type=j...  4.99 us
    dot_general x1, matrix products, local(): jnp.einsum('tji,tjf->tif', masked_tiles, chosen, preferred_element_type=j...  4.98 us
  transfers between devices with their start and end apart: 19, of which 4 were waited for; matrix products, arithmetic and copies ran while one was open for 26% of the time, Pallas kernels for 0%

profile of v1, /device:TPU:0, one launch (start us, length us, event | category | flops | bytes accessed | tf_op | source)
XLA Modules:
  0.0 246.6 jit_solution(8119187855748518487)
XLA Ops:
  7.2 0.7 fusion.6
  7.9 2.6 %gather_fusion = bf16[16,128,256]{2,1,0:T(8,128)(2,1)} fusion(bf16[4,128,256]{2,1,0:T(8,128)(2,1)} %bitcast.54, s32[1024]{0:T(1024)S(1)} %pad_clamp_fusion.3), kind=kCustom, calls=%fused_computation | custom fusion | bytes 2097216 | tf_op jit(solution)/shard_map/gather | solution.py:52
  10.5 8.5 %all-to-all-start = ((bf16[16,128,256]{2,1,0:T(8,128)(2,1)}), bf16[16,128,256]{2,1,0:T(8,128)(2,1)}, u32[]{:S(2)}, u32[]{:S(2)}) async-start(bf16[16,128,256]{2,1,0:T(8,128)(2,1)} %gather_fusion), calls=%async_computation | async-start | bytes 2097152 | tf_op jit(solution)/shard_map/all_to_all | solution.py:53
  19.0 0.0 reduce-scatter.3.cloned.1.call-start
  19.8 0.3 convolution_convert_fusion
  20.0 2.2 all_gather.6
  22.2 0.7 gather_fusion.2
  23.0 5.0 %fusion = f32[40,128,256]{2,1,0:T(8,128)} fusion(bf16[40,128,256]{2,1,0:T(8,128)(2,1)S(1)} %gather_fusion.2, bf16[40,128,128]{2,1,0:T(8,128)(2,1)} %param.11, bf16[40]{0:T(256)(128)(2,1)S(1)} %compare_convert_fusion), kind=kOutput, calls=%fused_computation.11 | convolution fusion | flops 336199680 | bytes 9175120 | tf_op jit(solution)/shard_map/tji,tjf->tif/dot_general | solution.py:70
  28.0 0.3 broadcast_in_dim.25
  28.2 0.4 copy-done.12
  28.6 9.1 %scatter_fusion.1 = f32[20,128,256]{2,1,0:T(8,128)S(1)} fusion(f32[20,128,256]{2,1,0:T(8,128)S(1)} %broadcast_in_dim.25, s32[40]{0:T(128)S(1)} %copy-done.12, f32[40,128,256]{2,1,0:T(8,128)} %fusion), kind=kCustom, calls=%fused_computation.5 | custom fusion | flops 1310720 | bytes 15728800 | tf_op jit(solution)/shard_map/scatter-add | solution.py:73
  37.7 1.6 slice.17
  39.3 2.8 %constant_dynamic-slice_fusion = (f32[1,128,256]{2,1,0:T(8,128)}, f32[1,128,256]{2,1,0:T(8,128)}, f32[1,128,256]{2,1,0:T(8,128)}, f32[1,128,256]{2,1,0:T(8,128)}...) fusion(f32[16,128,256]{2,1,0:T(8,128)} %slice.17, ...), kind=kLoop, calls=%fused_computation.37 | loop fusion | bytes 3932220 | tf_op jit(solution)/shard_map/squeeze | solution.py:34
  42.1 1.9 collective-permute-start
  44.0 1.5 collective-permute-start.1
  45.5 0.2 collective-permute-start.2
  45.6 1.9 collective-permute-start.3
  47.5 1.5 collective-permute-start.4
  49.0 1.6 bitcast_dynamic-update-slice_fusion.15
  50.6 2.4 collective-permute-start.5
  53.0 1.6 bitcast_dynamic-update-slice_fusion.14
  54.6 0.2 collective-permute-start.6
  54.8 1.6 bitcast_dynamic-update-slice_fusion.13
  56.4 1.4 pad_maximum_fusion
  57.7 2.4 gather_fusion.1
  60.1 5.0 %fusion.2 = f32[40,128,256]{2,1,0:T(8,128)} fusion(bf16[40,128,256]{2,1,0:T(8,128)(2,1)} %gather_fusion.1, bf16[40,128,128]{2,1,0:T(8,128)(2,1)S(1)} %copy-done.2, bf16[40]{0:T(256)(128)(2,1)S(1)} %compare_convert_fusion), kind=kOutput, calls=%fused_computation.13 | convolution fusion | flops 336199680 | bytes 9175120 | tf_op jit(solution)/shard_map/tij,tjf->tif/dot_general | solution.py:59
  65.1 0.1 broadcast_in_dim.22
  65.2 9.0 %scatter_fusion = f32[8,128,256]{2,1,0:T(8,128)S(1)} fusion(f32[8,128,256]{2,1,0:T(8,128)S(1)} %broadcast_in_dim.22, s32[40]{0:T(128)S(1)} %copy-done.13, f32[40,128,256]{2,1,0:T(8,128)} %fusion.2), kind=kCustom, calls=%fused_computation.4 | custom fusion | flops 1310720 | bytes 15728800 | tf_op jit(solution)/shard_map/scatter-add | solution.py:60
  74.3 0.9 copy-done.1
  75.3 0.0 reduce-scatter.5.cloned.1.call-start
  75.3 2.8 %collective-permute-start.7 = (f32[1,128,256]{2,1,0:T(8,128)S(1)}, f32[1,128,256]{2,1,0:T(8,128)S(1)}, u32[]{:S(2)}, u32[]{:S(2)}) collective-permute-start(f32[1,128,256]{2,1,0:T(8,128)S(1)} %copy-done.11), channel_id=1, source_target_pairs={{0,16},{2,18},{4,20},{6,22},{8,24},{10,26},{12,28},{14,30},{16,0},... | collective-permute-start | bytes 393224 | tf_op jit(solution)/shard_map/ppermute | solution.py:35
  78.2 1.6 bitcast_dynamic-update-slice_fusion.12
  79.7 1.4 collective-permute-start.8
  81.2 1.6 bitcast_dynamic-update-slice_fusion.11
  82.7 3.3 %collective-permute-start.9 = (f32[1,128,256]{2,1,0:T(8,128)S(1)}, f32[1,128,256]{2,1,0:T(8,128)S(1)}, u32[]{:S(2)}, u32[]{:S(2)}) collective-permute-start(f32[1,128,256]{2,1,0:T(8,128)S(1)} %copy-done.9), channel_id=1, source_target_pairs={{0,20},{2,22},{4,16},{6,18},{8,28},{10,30},{12,24},{14,26},{16,4},... | collective-permute-start | bytes 393224 | tf_op jit(solution)/shard_map/ppermute | solution.py:35
  86.0 1.6 bitcast_dynamic-update-slice_fusion.10
  87.6 0.2 collective-permute-start.10
  87.8 1.6 bitcast_dynamic-update-slice_fusion.9
  89.3 3.7 %collective-permute-start.11 = (f32[1,128,256]{2,1,0:T(8,128)S(1)}, f32[1,128,256]{2,1,0:T(8,128)S(1)}, u32[]{:S(2)}, u32[]{:S(2)}) collective-permute-start(f32[1,128,256]{2,1,0:T(8,128)S(1)} %copy-done.7), channel_id=1, source_target_pairs={{0,24},{2,26},{4,28},{6,30},{8,16},{10,18},{12,20},{14,22},{16,8},... | collective-permute-start | bytes 393224 | tf_op jit(solution)/shard_map/ppermute | solution.py:35
  93.0 1.6 bitcast_dynamic-update-slice_fusion.8
  94.6 4.1 %collective-permute-start.12 = (f32[1,128,256]{2,1,0:T(8,128)S(1)}, f32[1,128,256]{2,1,0:T(8,128)S(1)}, u32[]{:S(2)}, u32[]{:S(2)}) collective-permute-start(f32[1,128,256]{2,1,0:T(8,128)S(1)} %copy-done.6), channel_id=1, source_target_pairs={{0,26},{2,24},{4,30},{6,28},{8,18},{10,16},{12,22},{14,20},{16,10}... | collective-permute-start | bytes 393224 | tf_op jit(solution)/shard_map/ppermute | solution.py:35
  98.7 0.7 bitcast_dynamic-update-slice_fusion.7
  99.4 0.6 collective-permute-done.8
  100.0 4.0 %collective-permute-start.13 = (f32[1,128,256]{2,1,0:T(8,128)S(1)}, f32[1,128,256]{2,1,0:T(8,128)S(1)}, u32[]{:S(2)}, u32[]{:S(2)}) collective-permute-start(f32[1,128,256]{2,1,0:T(8,128)S(1)} %copy-done.5), channel_id=1, source_target_pairs={{0,28},{2,30},{4,24},{6,26},{8,20},{10,22},{12,16},{14,18},{16,12}... | collective-permute-start | bytes 393224 | tf_op jit(solution)/shard_map/ppermute | solution.py:35
  104.0 0.7 bitcast_dynamic-update-slice_fusion.6
  104.7 5.6 %collective-permute-start.14 = (f32[1,128,256]{2,1,0:T(8,128)S(1)}, f32[1,128,256]{2,1,0:T(8,128)S(1)}, u32[]{:S(2)}, u32[]{:S(2)}) collective-permute-start(f32[1,128,256]{2,1,0:T(8,128)S(1)} %copy-done.4), channel_id=1, source_target_pairs={{0,30},{2,28},{4,26},{6,24},{8,22},{10,20},{12,18},{14,16},{16,14}... | collective-permute-start | bytes 393224 | tf_op jit(solution)/shard_map/ppermute | solution.py:35
  110.3 0.7 bitcast_dynamic-update-slice_fusion.5
  111.0 3.0 %collective-permute-done.10 = f32[1,128,256]{2,1,0:T(8,128)S(1)} collective-permute-done((f32[1,128,256]{2,1,0:T(8,128)S(1)}, f32[1,128,256]{2,1,0:T(8,128)S(1)}, u32[]{:S(2)}, u32[]{:S(2)}) %collective-permute-start.10) | collective-permute-done | bytes 131104 | tf_op jit(solution)/shard_map/ppermute | solution.py:35
  113.9 0.7 bitcast_dynamic-update-slice_fusion.4
  114.6 0.7 bitcast_dynamic-update-slice_fusion.3
  115.3 1.1 convert_element_type.20
  116.4 1.0 convolution_multiply_fusion
  117.4 0.0 all-reduce.2.cloned.1.call-start
  117.4 0.7 bitcast_dynamic-update-slice_fusion.2
  118.1 0.7 bitcast_dynamic-update-slice_fusion.1
  118.7 0.7 bitcast_dynamic-update-slice_fusion
  119.4 2.3 gather_fusion.3
  121.7 2.2 scatter_fusion.2
  123.9 0.7 convert_element_type.23
  124.6 0.5 reduce-scatter.5.cloned.1.call-done
  125.2 0.9 convolution_convert_fusion.1
  126.1 111.1 %all-reduce.2.cloned.1.call-done = f32[128,256]{1,0:T(8,128)} async-done(((f32[128,256]{1,0:T(8,128)}), f32[128,256]{1,0:T(8,128)}) %all-reduce.2.cloned.1.call-update) | async-done | bytes 131088 | tf_op jit(solution)/shard_map/psum | solution.py:84
  237.2 2.2 all_gather.7
  239.4 0.7 copy.35
  (55 shorter events, 0.2 us)
Async XLA Ops:
  7.2 12.6 %copy-start = (bf16[512,256]{1,0:T(8,128)(2,1)S(1)}, bf16[512,256]{1,0:T(8,128)(2,1)}, u32[]{:S(2)}) copy-start(bf16[512,256]{1,0:T(8,128)(2,1)} %param.10) | copy-start | bytes 786436
  7.9 11.9 %copy-start.3 = (bf16[256,256]{1,0:T(8,128)(2,1)S(1)}, bf16[256,256]{1,0:T(8,128)(2,1)}, u32[]{:S(2)}) copy-start(bf16[256,256]{1,0:T(8,128)(2,1)} %param.9) | copy-start | bytes 393220
  10.5 11.8 %copy-start.13 = (s32[40]{0:T(128)S(1)}, s32[40]{0:T(128)}, u32[]{:S(2)}) copy-start(s32[40]{0:T(128)} %param.12) | copy-start | bytes 484
  10.5 45.9 %all-to-all-start = ((bf16[16,128,256]{2,1,0:T(8,128)(2,1)}), bf16[16,128,256]{2,1,0:T(8,128)(2,1)}, u32[]{:S(2)}, u32[]{:S(2)}) async-start(bf16[16,128,256]{2,1,0:T(8,128)(2,1)} %gather_fusion), calls=%async_computation | async-start | bytes 2097152 | tf_op jit(solution)/shard_map/all_to_all | solution.py:53
  19.0 96.3 %reduce-scatter.3.cloned.1.call-start = ((), (), s32[]{:S(2)}) async-start(), calls=%async_computation.3 | async-start | bytes 1572864 | tf_op jit(solution)/shard_map/reduce_scatter | solution.py:61
  28.0 0.7 copy-start.12
  42.1 8.6 %collective-permute-start = (f32[1,128,256]{2,1,0:T(8,128)}, f32[1,128,256]{2,1,0:T(8,128)}, u32[]{:S(2)}, u32[]{:S(2)}) collective-permute-start(f32[1,128,256]{2,1,0:T(8,128)} %get-tuple-element.17), channel_id=1, source_target_pairs={{0,2},{2,0},{4,6},{6,4},{8,10},{10,8},{12,14},{14,12},{16,18},{18,... | collective-permute-start | bytes 393224 | tf_op jit(solution)/shard_map/ppermute | solution.py:35
  44.0 10.6 %collective-permute-start.1 = (f32[1,128,256]{2,1,0:T(8,128)}, f32[1,128,256]{2,1,0:T(8,128)}, u32[]{:S(2)}, u32[]{:S(2)}) collective-permute-start(f32[1,128,256]{2,1,0:T(8,128)} %get-tuple-element.16), channel_id=1, source_target_pairs={{0,4},{2,6},{4,0},{6,2},{8,12},{10,14},{12,8},{14,10},{16,20},{18,... | collective-permute-start | bytes 393224 | tf_op jit(solution)/shard_map/ppermute | solution.py:35
  45.5 29.9 %collective-permute-start.2 = (f32[1,128,256]{2,1,0:T(8,128)}, f32[1,128,256]{2,1,0:T(8,128)}, u32[]{:S(2)}, u32[]{:S(2)}) collective-permute-start(f32[1,128,256]{2,1,0:T(8,128)} %get-tuple-element.15), channel_id=1, source_target_pairs={{0,6},{2,4},{4,2},{6,0},{8,14},{10,12},{12,10},{14,8},{16,22},{18,... | collective-permute-start | bytes 393224 | tf_op jit(solution)/shard_map/ppermute | solution.py:35
  45.6 34.1 %collective-permute-start.3 = (f32[1,128,256]{2,1,0:T(8,128)}, f32[1,128,256]{2,1,0:T(8,128)}, u32[]{:S(2)}, u32[]{:S(2)}) collective-permute-start(f32[1,128,256]{2,1,0:T(8,128)} %get-tuple-element.14), channel_id=1, source_target_pairs={{0,8},{2,10},{4,12},{6,14},{8,0},{10,2},{12,4},{14,6},{16,24},{18,... | collective-permute-start | bytes 393224 | tf_op jit(solution)/shard_map/ppermute | solution.py:35
  47.5 35.2 %collective-permute-start.4 = (f32[1,128,256]{2,1,0:T(8,128)}, f32[1,128,256]{2,1,0:T(8,128)}, u32[]{:S(2)}, u32[]{:S(2)}) collective-permute-start(f32[1,128,256]{2,1,0:T(8,128)} %get-tuple-element.13), channel_id=1, source_target_pairs={{0,10},{2,8},{4,14},{6,12},{8,2},{10,0},{12,6},{14,4},{16,26},{18,... | collective-permute-start | bytes 393224 | tf_op jit(solution)/shard_map/ppermute | solution.py:35
  50.6 36.9 %collective-permute-start.5 = (f32[1,128,256]{2,1,0:T(8,128)}, f32[1,128,256]{2,1,0:T(8,128)}, u32[]{:S(2)}, u32[]{:S(2)}) collective-permute-start(f32[1,128,256]{2,1,0:T(8,128)} %get-tuple-element.12), channel_id=1, source_target_pairs={{0,12},{2,14},{4,8},{6,10},{8,4},{10,6},{12,0},{14,2},{16,28},{18,... | collective-permute-start | bytes 393224 | tf_op jit(solution)/shard_map/ppermute | solution.py:35
  54.6 34.7 %collective-permute-start.6 = (f32[1,128,256]{2,1,0:T(8,128)}, f32[1,128,256]{2,1,0:T(8,128)}, u32[]{:S(2)}, u32[]{:S(2)}) collective-permute-start(f32[1,128,256]{2,1,0:T(8,128)} %get-tuple-element.11), channel_id=1, source_target_pairs={{0,14},{2,12},{4,10},{6,8},{8,6},{10,4},{12,2},{14,0},{16,30},{18,... | collective-permute-start | bytes 393224 | tf_op jit(solution)/shard_map/ppermute | solution.py:35
  57.7 2.4 copy-start.2
  65.2 10.2 %copy-start.11 = (f32[1,128,256]{2,1,0:T(8,128)S(1)}, f32[1,128,256]{2,1,0:T(8,128)}, u32[]{:S(2)}) copy-start(f32[1,128,256]{2,1,0:T(8,128)} %get-tuple-element.10) | copy-start | bytes 393220
  65.2 14.5 %copy-start.10 = (f32[1,128,256]{2,1,0:T(8,128)S(1)}, f32[1,128,256]{2,1,0:T(8,128)}, u32[]{:S(2)}) copy-start(f32[1,128,256]{2,1,0:T(8,128)} %get-tuple-element.9) | copy-start | bytes 393220
  65.2 17.5 %copy-start.9 = (f32[1,128,256]{2,1,0:T(8,128)S(1)}, f32[1,128,256]{2,1,0:T(8,128)}, u32[]{:S(2)}) copy-start(f32[1,128,256]{2,1,0:T(8,128)} %get-tuple-element.8) | copy-start | bytes 393220
  65.2 22.4 %copy-start.8 = (f32[1,128,256]{2,1,0:T(8,128)S(1)}, f32[1,128,256]{2,1,0:T(8,128)}, u32[]{:S(2)}) copy-start(f32[1,128,256]{2,1,0:T(8,128)} %get-tuple-element.7) | copy-start | bytes 393220
  74.3 1.0 copy-start.1
  74.3 15.1 %copy-start.7 = (f32[1,128,256]{2,1,0:T(8,128)S(1)}, f32[1,128,256]{2,1,0:T(8,128)}, u32[]{:S(2)}) copy-start(f32[1,128,256]{2,1,0:T(8,128)} %get-tuple-element.6) | copy-start | bytes 393220
  74.3 20.3 %copy-start.6 = (f32[1,128,256]{2,1,0:T(8,128)S(1)}, f32[1,128,256]{2,1,0:T(8,128)}, u32[]{:S(2)}) copy-start(f32[1,128,256]{2,1,0:T(8,128)} %get-tuple-element.5) | copy-start | bytes 393220
  74.3 25.7 %copy-start.5 = (f32[1,128,256]{2,1,0:T(8,128)S(1)}, f32[1,128,256]{2,1,0:T(8,128)}, u32[]{:S(2)}) copy-start(f32[1,128,256]{2,1,0:T(8,128)} %get-tuple-element.4) | copy-start | bytes 393220
  74.3 30.4 %copy-start.4 = (f32[1,128,256]{2,1,0:T(8,128)S(1)}, f32[1,128,256]{2,1,0:T(8,128)}, u32[]{:S(2)}) copy-start(f32[1,128,256]{2,1,0:T(8,128)} %get-tuple-element.3) | copy-start | bytes 393220
  75.3 49.9 %reduce-scatter.5.cloned.1.call-start = ((), (), s32[]{:S(2)}) async-start(), calls=%async_computation.4 | async-start | bytes 393216 | tf_op jit(solution)/shard_map/reduce_scatter | solution.py:83
  75.3 19.2 %collective-permute-start.7 = (f32[1,128,256]{2,1,0:T(8,128)S(1)}, f32[1,128,256]{2,1,0:T(8,128)S(1)}, u32[]{:S(2)}, u32[]{:S(2)}) collective-permute-start(f32[1,128,256]{2,1,0:T(8,128)S(1)} %copy-done.11), channel_id=1, source_target_pairs={{0,16},{2,18},{4,20},{6,22},{8,24},{10,26},{12,28},{14,30},{16,0},... | collective-permute-start | bytes 393224 | tf_op jit(solution)/shard_map/ppermute | solution.py:35
  79.7 20.3 %collective-permute-start.8 = (f32[1,128,256]{2,1,0:T(8,128)S(1)}, f32[1,128,256]{2,1,0:T(8,128)S(1)}, u32[]{:S(2)}, u32[]{:S(2)}) collective-permute-start(f32[1,128,256]{2,1,0:T(8,128)S(1)} %copy-done.10), channel_id=1, source_target_pairs={{0,18},{2,16},{4,22},{6,20},{8,26},{10,24},{12,30},{14,28},{16,2},... | collective-permute-start | bytes 393224 | tf_op jit(solution)/shard_map/ppermute | solution.py:35
  82.7 22.0 %collective-permute-start.9 = (f32[1,128,256]{2,1,0:T(8,128)S(1)}, f32[1,128,256]{2,1,0:T(8,128)S(1)}, u32[]{:S(2)}, u32[]{:S(2)}) collective-permute-start(f32[1,128,256]{2,1,0:T(8,128)S(1)} %copy-done.9), channel_id=1, source_target_pairs={{0,20},{2,22},{4,16},{6,18},{8,28},{10,30},{12,24},{14,26},{16,4},... | collective-permute-start | bytes 393224 | tf_op jit(solution)/shard_map/ppermute | solution.py:35
  87.6 26.3 %collective-permute-start.10 = (f32[1,128,256]{2,1,0:T(8,128)S(1)}, f32[1,128,256]{2,1,0:T(8,128)S(1)}, u32[]{:S(2)}, u32[]{:S(2)}) collective-permute-start(f32[1,128,256]{2,1,0:T(8,128)S(1)} %copy-done.8), channel_id=1, source_target_pairs={{0,22},{2,20},{4,18},{6,16},{8,30},{10,28},{12,26},{14,24},{16,6},... | collective-permute-start | bytes 393224 | tf_op jit(solution)/shard_map/ppermute | solution.py:35
  89.3 25.3 %collective-permute-start.11 = (f32[1,128,256]{2,1,0:T(8,128)S(1)}, f32[1,128,256]{2,1,0:T(8,128)S(1)}, u32[]{:S(2)}, u32[]{:S(2)}) collective-permute-start(f32[1,128,256]{2,1,0:T(8,128)S(1)} %copy-done.7), channel_id=1, source_target_pairs={{0,24},{2,26},{4,28},{6,30},{8,16},{10,18},{12,20},{14,22},{16,8},... | collective-permute-start | bytes 393224 | tf_op jit(solution)/shard_map/ppermute | solution.py:35
  94.6 22.8 %collective-permute-start.12 = (f32[1,128,256]{2,1,0:T(8,128)S(1)}, f32[1,128,256]{2,1,0:T(8,128)S(1)}, u32[]{:S(2)}, u32[]{:S(2)}) collective-permute-start(f32[1,128,256]{2,1,0:T(8,128)S(1)} %copy-done.6), channel_id=1, source_target_pairs={{0,26},{2,24},{4,30},{6,28},{8,18},{10,16},{12,22},{14,20},{16,10}... | collective-permute-start | bytes 393224 | tf_op jit(solution)/shard_map/ppermute | solution.py:35
  100.0 18.1 %collective-permute-start.13 = (f32[1,128,256]{2,1,0:T(8,128)S(1)}, f32[1,128,256]{2,1,0:T(8,128)S(1)}, u32[]{:S(2)}, u32[]{:S(2)}) collective-permute-start(f32[1,128,256]{2,1,0:T(8,128)S(1)} %copy-done.5), channel_id=1, source_target_pairs={{0,28},{2,30},{4,24},{6,26},{8,20},{10,22},{12,16},{14,18},{16,12}... | collective-permute-start | bytes 393224 | tf_op jit(solution)/shard_map/ppermute | solution.py:35
  104.7 14.0 %collective-permute-start.14 = (f32[1,128,256]{2,1,0:T(8,128)S(1)}, f32[1,128,256]{2,1,0:T(8,128)S(1)}, u32[]{:S(2)}, u32[]{:S(2)}) collective-permute-start(f32[1,128,256]{2,1,0:T(8,128)S(1)} %copy-done.4), channel_id=1, source_target_pairs={{0,30},{2,28},{4,26},{6,24},{8,22},{10,20},{12,18},{14,16},{16,14}... | collective-permute-start | bytes 393224 | tf_op jit(solution)/shard_map/ppermute | solution.py:35
  117.4 119.8 %all-reduce.2.cloned.1.call-start = ((), (), s32[]{:S(2)}) async-start(), calls=%async_computation.5 | async-start | bytes 262144 | tf_op jit(solution)/shard_map/psum | solution.py:84
  119.4 2.3 copy-start.14
Sparse Core Ops, SparseCore 0:
  75.4 9.5 reduce-scatter.2
  117.5 7.6 reduce-scatter.4
  130.6 106.5 all-reduce.1
